TPU v7x, 256 devices: a whole 4x4x8 slice. The times are simulated.
256 devices in a mesh: grid: 64 (over x, z, core), chan: 4 (over y).
Axes of the slice: x: 4, y: 4, z: 8, core: 2. Of those that a mesh axis runs over, the one named last changes fastest.
Arguments:
- volt: float32 [2, 128, 4096, 512], P(None, None, 'grid', 'chan'), may hold values from -13 to 13
- placement: int32 [4096], P('grid'), may hold values from 0 to 63, as said below
- flags: int32 [4096], P('grid'), may hold values 0 or 1
Outputs:
- sky_image: float32 [64, 64], P('chan', 'grid')
Inputs may be any that keep to these rules, and one draw needn't show every extreme that they name: `placement`: within every grid row r, antennas r * 64 to (r + 1) * 64 - 1 take each column 0 to 63 exactly once.
All inputs are finite; a program needn't handle non-finite values. No bound on the sum of `flags` on one device may be relied on, other than what follows from the above.
Results may differ from a plain program's by a relative error of at most 0.0001.
Values sent between devices are 32-bit elements; how exact they have to be, the bound alone decides.
A program may use at most 128 MiB of HBM per device.

v0:
```python
import math

import jax
import jax.numpy as jnp
import numpy as np
from jax import lax
from jax.experimental import pallas as pl
from jax.experimental.pallas import tpu as pltpu
from jax.sharding import PartitionSpec as P

NROW = 64
GRID_COLUMNS = 64
CHANNELS = 512
TIMES = 128
LANES = 128
CHUNKS = 8
AHEAD = 4
MESH = pl.DeviceIdType.MESH
HIGHEST = lax.Precision.HIGHEST


def fourier_matrix():
    ids = np.outer(np.arange(NROW), np.arange(NROW)) % NROW
    turned = ids * (2.0 * math.pi / NROW)
    cos, sin = np.cos(turned), np.sin(turned)
    return np.block([[cos, sin], [-sin, cos]]).astype(np.float32)


def grid_peer(me, j):
    z_rank = j // 8
    half = (z_rank + 1) // 2
    dz = 4 + half * (1 - 2 * (z_rank % 2))
    dc = 1 - (j // 4) % 2
    dx = 3 - j % 4
    x, z, c = me // 16, (me // 2) % 8, me % 2
    return ((x + dx) % 4) * 16 + ((z + dz) % 8) * 2 + (c + dc) % 2


def kernel(
    volt, placement, flags, table, out,
    staged, rows, cols, table_here, mix, power, parts,
    load_sem, table_sem, send_sem, recv_sem, part_send, part_recv,
):
    me = lax.axis_index("grid")
    group = lax.axis_index("chan")
    grid_count = NROW
    chan_count = parts.shape[0] + 1
    times = staged.shape[2]
    share = out.shape[0]

    loads = [
        pltpu.make_async_copy(volt.at[:, pl.ds(k * times, times)], staged.at[k], load_sem.at[k])
        for k in range(CHUNKS)
    ]
    table_load = pltpu.make_async_copy(table, table_here, table_sem)
    table_load.start()
    for load in loads:
        load.start()

    barrier = pltpu.get_barrier_semaphore()

    def greet(j, carry):
        pl.semaphore_signal(barrier, inc=1, device_id={"grid": grid_peer(me, j)}, device_id_type=MESH)
        return carry

    lax.fori_loop(0, grid_count - 1, greet, 0)
    for d in range(1, chan_count):
        pl.semaphore_signal(
            barrier, inc=1, device_id={"chan": lax.rem(group + d, chan_count)}, device_id_type=MESH
        )

    position = lax.broadcasted_iota(jnp.int32, (GRID_COLUMNS, GRID_COLUMNS), 0)
    pick = jnp.where(position == placement[...], flags[...].astype(jnp.float32), 0.0)
    none = jnp.zeros_like(pick)
    pick = jnp.concatenate(
        [jnp.concatenate([pick, none], axis=1), jnp.concatenate([none, pick], axis=1)], axis=0
    )
    table_load.wait()
    mix[...] = jnp.dot(table_here[...], pick, precision=HIGHEST, preferred_element_type=jnp.float32)
    power[...] = jnp.zeros_like(power)

    def row_dft(k):
        def one_time(t, carry):
            x = staged[k, :, t].reshape(2 * GRID_COLUMNS, LANES)
            y = jnp.dot(mix[...], x, precision=HIGHEST, preferred_element_type=jnp.float32)
            rows[k, 2 * t] = y[:GRID_COLUMNS]
            rows[k, 2 * t + 1] = y[GRID_COLUMNS:]
            return carry

        lax.fori_loop(0, times, one_time, 0)

    def send(k):
        def one_peer(j, carry):
            peer = grid_peer(me, j)
            pltpu.make_async_remote_copy(
                src_ref=rows.at[k, :, peer],
                dst_ref=cols.at[k, :, me],
                send_sem=send_sem.at[k],
                recv_sem=recv_sem.at[k],
                device_id={"grid": peer},
                device_id_type=MESH,
            ).start()
            return carry

        lax.fori_loop(0, grid_count - 1, one_peer, 0)
        cols[k, :, pl.ds(me, 1)] = rows[k, :, pl.ds(me, 1)]

    def all_copies(k):
        return pltpu.make_async_remote_copy(
            src_ref=rows.at[k, :, pl.ds(0, grid_count - 1)],
            dst_ref=cols.at[k, :, pl.ds(0, grid_count - 1)],
            send_sem=send_sem.at[k],
            recv_sem=recv_sem.at[k],
            device_id={"grid": grid_peer(me, 0)},
            device_id_type=MESH,
        )

    def col_dft(k):
        def one_time(t, total):
            x = cols[k, pl.ds(2 * t, 2)].reshape(2 * NROW, LANES)
            y = jnp.dot(table_here[...], x, precision=HIGHEST, preferred_element_type=jnp.float32)
            return total + y * y

        power[...] += lax.fori_loop(0, times, one_time, jnp.zeros((2 * NROW, LANES), jnp.float32))

    loads[0].wait()
    row_dft(0)
    pl.semaphore_wait(barrier, grid_count - 1 + chan_count - 1)
    send(0)
    for k in range(1, AHEAD):
        loads[k].wait()
        row_dft(k)
        send(k)

    for k in range(CHUNKS):
        if k + AHEAD < CHUNKS:
            loads[k + AHEAD].wait()
            row_dft(k + AHEAD)
            send(k + AHEAD)
        all_copies(k).wait_recv()
        col_dft(k)

    power[:NROW] = power[:NROW] + power[NROW:]
    copies = []
    for d in range(1, chan_count):
        peer = lax.rem(group + d, chan_count)
        copies.append(
            pltpu.make_async_remote_copy(
                src_ref=power.at[pl.ds(pl.multiple_of(peer * share, share), share)],
                dst_ref=parts.at[d - 1],
                send_sem=part_send.at[d - 1],
                recv_sem=part_recv.at[d - 1],
                device_id={"chan": peer},
                device_id_type=MESH,
            )
        )
        copies[-1].start()
    for k in range(CHUNKS):
        all_copies(k).wait_send()
    total = power[pl.ds(pl.multiple_of(group * share, share), share)]
    for d in range(1, chan_count):
        copies[d - 1].wait()
        total = total + parts[d - 1]
    out[...] = jnp.sum(total, axis=1, keepdims=True) * (1.0 / (TIMES * CHANNELS * NROW * GRID_COLUMNS))


def on_device(volt, placement, flags):
    times = volt.shape[1] // CHUNKS
    chan_count = lax.axis_size("chan")
    share = NROW // chan_count
    any_space = pl.BlockSpec(memory_space=pl.ANY)
    vmem = pl.BlockSpec(memory_space=pltpu.VMEM)
    return pl.pallas_call(
        kernel,
        name="sky",
        out_shape=jax.ShapeDtypeStruct((share, 1), jnp.float32),
        in_specs=[any_space, vmem, vmem, any_space],
        out_specs=vmem,
        scratch_shapes=[
            pltpu.VMEM((CHUNKS, 2, times, GRID_COLUMNS, LANES), jnp.float32),
            pltpu.VMEM((CHUNKS, 2 * times, GRID_COLUMNS, LANES), jnp.float32),
            pltpu.VMEM((CHUNKS, 2 * times, NROW, LANES), jnp.float32),
            pltpu.VMEM((2 * NROW, 2 * NROW), jnp.float32),
            pltpu.VMEM((2 * GRID_COLUMNS, 2 * GRID_COLUMNS), jnp.float32),
            pltpu.VMEM((2 * NROW, LANES), jnp.float32),
            pltpu.VMEM((chan_count - 1, share, LANES), jnp.float32),
            pltpu.SemaphoreType.DMA((CHUNKS,)),
            pltpu.SemaphoreType.DMA,
            pltpu.SemaphoreType.DMA((CHUNKS,)),
            pltpu.SemaphoreType.DMA((CHUNKS,)),
            pltpu.SemaphoreType.DMA((chan_count - 1,)),
            pltpu.SemaphoreType.DMA((chan_count - 1,)),
        ],
        compiler_params=pltpu.CompilerParams(
            collective_id=0, has_side_effects=True, vmem_limit_bytes=60 * 2**20
        ),
    )(
        volt,
        placement.reshape(1, GRID_COLUMNS),
        flags.reshape(1, GRID_COLUMNS),
        jnp.asarray(fourier_matrix()),
    )


def solution(mesh):
    return jax.shard_map(
        on_device,
        mesh=mesh,
        in_specs=(P(None, None, "grid", "chan"), P("grid"), P("grid")),
        out_specs=P("chan", "grid"),
        check_vma=False,
    )
```

profile of v0, /device:TPU:1, one launch (start us, length us, event | category | flops | bytes accessed | tf_op | source)
XLA Modules:
  0.0 206.1 jit_solution(2791876470322781882)
XLA Ops:
  0.0 204.8 %sky.1 = f32[16,1]{1,0:T(8,128)} custom-call(f32[2,128,64,128]{3,2,1,0:T(8,128)} %volt.1, s32[1,64]{1,0:T(1,128)} %bitcast.2, s32[1,64]{1,0:T(1,128)} %bitcast.3, f32[128,128]{1,0:T(8,128)} %constant.2.clone.table), custom_call_target="tpu_custom_call" | custom-call | tf_op jit(solution)/shard_map/sky/pallas_call | solution.py:173
  204.8 1.3 copy.5
where the time goes:
time: 206 us
  Pallas kernels  205 us (100%)
    pallas_call x1, Pallas kernels, on_device(): pl.pallas_call(kernel, name='sky', out_shape=jax.ShapeDtypeStruct((share,...  205 us

commit v1 on v0

v1 whole, which is shorter than its diff:
```python
import math

import jax
import jax.numpy as jnp
import numpy as np
from jax import lax
from jax.experimental import pallas as pl
from jax.experimental.pallas import tpu as pltpu
from jax.sharding import PartitionSpec as P

NROW = 64
GRID_COLUMNS = 64
CHANNELS = 512
TIMES = 128
LANES = 128
SIZES = (8, 8, 16, 16, 16, 16, 16, 16, 8, 4, 4)
STARTS = tuple(sum(SIZES[:k]) for k in range(len(SIZES)))
AHEAD = 64
UNROLL = 8
MESH = pl.DeviceIdType.MESH
HIGHEST = lax.Precision.HIGHEST


def fourier_matrix():
    ids = np.outer(np.arange(NROW), np.arange(NROW)) % NROW
    turned = ids * (2.0 * math.pi / NROW)
    cos, sin = np.cos(turned), np.sin(turned)
    return np.block([[cos, sin], [-sin, cos]]).astype(np.float32)


def z_ring_peer(me, j):
    rank = j // 2
    half = (rank + 1) // 2
    dz = 4 + half * (1 - 2 * (rank % 2))
    dc = 1 - j % 2
    x, z, c = me // 16, (me // 2) % 8, me % 2
    return x * 16 + ((z + dz) % 8) * 2 + (c + dc) % 2


def other_peer(me, j):
    rank = j // 6
    half = (rank + 1) // 2
    dz = 4 + half * (1 - 2 * (rank % 2))
    dc = 1 - (j // 3) % 2
    dx = 3 - j % 3
    x, z, c = me // 16, (me // 2) % 8, me % 2
    return ((x + dx) % 4) * 16 + ((z + dz) % 8) * 2 + (c + dc) % 2


def line_peer(me, d):
    return (me + 16 * d) % 64


def kernel(
    volt, placement, flags, table, out,
    staged, rows, cols, table_here, placement_here, flags_here, mix, power, parts,
    load_sem, small_sem, send_sem, recv_sem, ring_sem, part_send, part_recv,
):
    me = lax.axis_index("grid")
    group = lax.axis_index("chan")
    chan_count = parts.shape[0] + 1
    share = parts.shape[1]
    chunks = len(SIZES)

    def signal(semaphore, peer):
        pl.semaphore_signal(semaphore, inc=1, device_id=peer, device_id_type=MESH)

    barrier = pltpu.get_barrier_semaphore()
    for j in range(15):
        signal(barrier, {"grid": z_ring_peer(me, j)})
    for d in (2, 1, 3):
        signal(barrier, {"grid": line_peer(me, d)})
    for d in range(1, chan_count):
        signal(barrier, {"chan": lax.rem(group + d, chan_count)})

    loads = [
        pltpu.make_async_copy(
            volt.at[:, pl.ds(STARTS[k], SIZES[k])], staged.at[:, pl.ds(STARTS[k], SIZES[k])], load_sem.at[k]
        )
        for k in range(chunks)
    ]
    small = [
        pltpu.make_async_copy(placement, placement_here, small_sem.at[0]),
        pltpu.make_async_copy(flags, flags_here, small_sem.at[1]),
        pltpu.make_async_copy(table, table_here, small_sem.at[2]),
    ]
    for load in small + loads[:2]:
        load.start()
    for load in small:
        load.wait()

    position = lax.broadcasted_iota(jnp.int32, (GRID_COLUMNS, GRID_COLUMNS), 0)
    pick = jnp.where(position == placement_here[...], flags_here[...].astype(jnp.float32), 0.0)
    none = jnp.zeros_like(pick)
    pick = jnp.concatenate(
        [jnp.concatenate([pick, none], axis=1), jnp.concatenate([none, pick], axis=1)], axis=0
    )
    mix[...] = jnp.dot(table_here[...], pick, precision=HIGHEST, preferred_element_type=jnp.float32)
    power[...] = jnp.zeros_like(power)

    def row_dft(k):
        def one_time(i, carry):
            t = STARTS[k] + i
            x = staged[:, t].reshape(2 * GRID_COLUMNS, LANES)
            y = jnp.dot(mix[...], x, precision=HIGHEST, preferred_element_type=jnp.float32)
            rows[2 * t] = y[:GRID_COLUMNS]
            rows[2 * t + 1] = y[GRID_COLUMNS:]
            return carry

        lax.fori_loop(0, SIZES[k], one_time, 0)

    def span(k):
        return pl.ds(2 * STARTS[k], 2 * SIZES[k])

    def send_to(k, peer):
        pltpu.make_async_remote_copy(
            src_ref=rows.at[span(k), peer],
            dst_ref=cols.at[span(k), me],
            send_sem=send_sem.at[k],
            recv_sem=recv_sem.at[k],
            device_id={"grid": peer},
            device_id_type=MESH,
        ).start()

    def send_ring(k):
        def one_peer(j, carry):
            send_to(k, z_ring_peer(me, j))
            return carry

        lax.fori_loop(0, 15, one_peer, 0, unroll=UNROLL)

    def send_others(k):
        def one_peer(j, carry):
            send_to(k, other_peer(me, j))
            return carry

        lax.fori_loop(0, 48, one_peer, 0, unroll=UNROLL)
        cols[span(k), pl.ds(me, 1)] = rows[span(k), pl.ds(me, 1)]

    def all_copies(k):
        return pltpu.make_async_remote_copy(
            src_ref=rows.at[span(k), pl.ds(0, NROW - 1)],
            dst_ref=cols.at[span(k), pl.ds(0, NROW - 1)],
            send_sem=send_sem.at[k],
            recv_sem=recv_sem.at[k],
            device_id={"grid": line_peer(me, 1)},
            device_id_type=MESH,
        )

    def col_dft(k):
        all_copies(k).wait_recv()

        def one_time(i, total):
            x = cols[pl.ds(2 * (STARTS[k] + i), 2)].reshape(2 * NROW, LANES)
            y = jnp.dot(table_here[...], x, precision=HIGHEST, preferred_element_type=jnp.float32)
            return total + y * y

        power[...] += lax.fori_loop(0, SIZES[k], one_time, jnp.zeros((2 * NROW, LANES), jnp.float32))

    loads[0].wait()
    for load in loads[2:]:
        load.start()
    row_dft(0)
    pl.semaphore_wait(barrier, 15 + 3 + chan_count - 1)
    for d in (2, 1, 3):
        signal(ring_sem, {"grid": line_peer(me, d)})
    send_ring(0)
    pl.semaphore_wait(ring_sem, 3)
    send_others(0)

    received = 0
    for k in range(1, chunks):
        while STARTS[k] - STARTS[received] >= AHEAD:
            col_dft(received)
            received += 1
        loads[k].wait()
        row_dft(k)
        send_ring(k)
        send_others(k)
    for k in range(received, chunks):
        col_dft(k)

    power[:NROW] = power[:NROW] + power[NROW:]
    copies = []
    for d in (2, 1, 3):
        peer = lax.rem(group + d, chan_count)
        copies.append(
            pltpu.make_async_remote_copy(
                src_ref=power.at[pl.ds(pl.multiple_of(peer * share, share), share)],
                dst_ref=parts.at[d - 1],
                send_sem=part_send.at[d - 1],
                recv_sem=part_recv.at[d - 1],
                device_id={"chan": peer},
                device_id_type=MESH,
            )
        )
        copies[-1].start()
    for k in range(chunks):
        all_copies(k).wait_send()
    for copy in copies:
        copy.wait()
    total = power[pl.ds(pl.multiple_of(group * share, share), share)]
    total = (total + parts[0]) + (parts[1] + parts[2])
    out[...] = jnp.sum(total.T, axis=0, keepdims=True) * (1.0 / (TIMES * CHANNELS * NROW * GRID_COLUMNS))


def on_device(volt, placement, flags):
    chan_count = lax.axis_size("chan")
    share = NROW // chan_count
    hbm = pl.BlockSpec(memory_space=pltpu.HBM)
    vmem = pl.BlockSpec(memory_space=pltpu.VMEM)
    image = pl.pallas_call(
        kernel,
        name="sky",
        out_shape=pltpu.VMEM((1, share), jnp.float32),
        in_specs=[hbm, hbm, hbm, hbm],
        out_specs=vmem,
        scratch_shapes=[
            pltpu.VMEM((2, TIMES, GRID_COLUMNS, LANES), jnp.float32),
            pltpu.VMEM((2 * TIMES, GRID_COLUMNS, LANES), jnp.float32),
            pltpu.VMEM((2 * TIMES, NROW, LANES), jnp.float32),
            pltpu.VMEM((2 * NROW, 2 * NROW), jnp.float32),
            pltpu.VMEM((1, GRID_COLUMNS), jnp.int32),
            pltpu.VMEM((1, GRID_COLUMNS), jnp.int32),
            pltpu.VMEM((2 * GRID_COLUMNS, 2 * GRID_COLUMNS), jnp.float32),
            pltpu.VMEM((2 * NROW, LANES), jnp.float32),
            pltpu.VMEM((chan_count - 1, share, LANES), jnp.float32),
            pltpu.SemaphoreType.DMA((len(SIZES),)),
            pltpu.SemaphoreType.DMA((3,)),
            pltpu.SemaphoreType.DMA((len(SIZES),)),
            pltpu.SemaphoreType.DMA((len(SIZES),)),
            pltpu.SemaphoreType.REGULAR,
            pltpu.SemaphoreType.DMA((chan_count - 1,)),
            pltpu.SemaphoreType.DMA((chan_count - 1,)),
        ],
        compiler_params=pltpu.CompilerParams(
            collective_id=0, has_side_effects=True, vmem_limit_bytes=60 * 2**20
        ),
    )(
        volt,
        placement.reshape(1, GRID_COLUMNS),
        flags.reshape(1, GRID_COLUMNS),
        jnp.asarray(fourier_matrix()),
    )
    return image.reshape(share, 1)


def solution(mesh):
    return jax.shard_map(
        on_device,
        mesh=mesh,
        in_specs=(P(None, None, "grid", "chan"), P("grid"), P("grid")),
        out_specs=P("chan", "grid"),
        check_vma=False,
    )
```

time: 206 us -> 199 us (0.966)
  Pallas kernels: 205 us -> 198 us
    pallas_call x1, Pallas kernels: 205 us -> 198 us  [on_device(): pl.pallas_call(kernel, name='sky', out_shape=pltpu.VMEM((1, share), jnp.f...]
where the time goes in v1:
time: 199 us
  Pallas kernels  198 us (99%)
    pallas_call x1, Pallas kernels, on_device(): pl.pallas_call(kernel, name='sky', out_shape=pltpu.VMEM((1, share), jnp.f...  198 us

profile of v1, /device:TPU:1, one launch (start us, length us, event | category | flops | bytes accessed | tf_op | source)
XLA Modules:
  0.0 198.5 jit_solution(3295627200880543850)
XLA Ops:
  0.0 198.0 %sky.1 = f32[1,16]{1,0:T(1,128)S(1)} custom-call(f32[2,128,64,128]{3,2,1,0:T(8,128)} %volt.1, s32[1,64]{1,0:T(1,128)} %bitcast.4, s32[1,64]{1,0:T(1,128)} %bitcast.5, f32[128,128]{1,0:T(8,128)} %constant.2.clone.table), custom_call_target="tpu_custom_call" | custom-call | tf_op jit(solution)/shard_map/sky/pallas_call | solution.py:212
  198.0 0.5 copy.6

commit v2 on v1

--- a/solution.py
+++ b/solution.py
@@ -13,7 +13,7 @@
 CHANNELS = 512
 TIMES = 128
 LANES = 128
-SIZES = (8, 8, 16, 16, 16, 16, 16, 16, 8, 4, 4)
+SIZES = (8, 8, 16, 16, 16, 16, 16, 16, 8, 4, 2, 2)
 STARTS = tuple(sum(SIZES[:k]) for k in range(len(SIZES)))
 AHEAD = 64
 UNROLL = 8
@@ -28,23 +28,35 @@
     return np.block([[cos, sin], [-sin, cos]]).astype(np.float32)
 
 
-def z_ring_peer(me, j):
+def at_offset(me, dx, dz, core):
+    x, z = me // 16, (me // 2) % 8
+    return ((x + dx) % 4) * 16 + ((z + dz) % 8) * 2 + core
+
+
+def near_peer(me, j):
     rank = j // 2
-    half = (rank + 1) // 2
-    dz = 4 + half * (1 - 2 * (rank % 2))
-    dc = 1 - j % 2
-    x, z, c = me // 16, (me // 2) % 8, me % 2
-    return x * 16 + ((z + dz) % 8) * 2 + (c + dc) % 2
+    return at_offset(me, 0, 2 - rank - rank // 2, j % 2)
+
+
+def far_peer(me, j):
+    return at_offset(me, 0, 3 + j // 2, j % 2)
+
+
+def core_mate(me):
+    return me + 1 - 2 * (me % 2)
 
 
 def other_peer(me, j):
     rank = j // 6
     half = (rank + 1) // 2
-    dz = 4 + half * (1 - 2 * (rank % 2))
-    dc = 1 - (j // 3) % 2
-    dx = 3 - j % 3
-    x, z, c = me // 16, (me // 2) % 8, me % 2
-    return ((x + dx) % 4) * 16 + ((z + dz) % 8) * 2 + (c + dc) % 2
+    return at_offset(me, 3 - j % 3, 4 + half * (1 - 2 * (rank % 2)), (j // 3) % 2)
+
+
+def last_peer(me, j):
+    core, rest = j // 31, j % 31
+    rank = rest // 4
+    half = (rank + 1) // 2
+    return at_offset(me, 3 - rest % 4, 4 + half * (1 - 2 * (rank % 2)), core)
 
 
 def line_peer(me, d):
@@ -54,7 +66,7 @@
 def kernel(
     volt, placement, flags, table, out,
     staged, rows, cols, table_here, placement_here, flags_here, mix, power, parts,
-    load_sem, small_sem, send_sem, recv_sem, ring_sem, part_send, part_recv,
+    load_sem, small_sem, send_sem, recv_sem, near_sem, ring_sem, part_send, part_recv,
 ):
     me = lax.axis_index("grid")
     group = lax.axis_index("chan")
@@ -64,14 +76,6 @@
 
     def signal(semaphore, peer):
         pl.semaphore_signal(semaphore, inc=1, device_id=peer, device_id_type=MESH)
-
-    barrier = pltpu.get_barrier_semaphore()
-    for j in range(15):
-        signal(barrier, {"grid": z_ring_peer(me, j)})
-    for d in (2, 1, 3):
-        signal(barrier, {"grid": line_peer(me, d)})
-    for d in range(1, chan_count):
-        signal(barrier, {"chan": lax.rem(group + d, chan_count)})
 
     loads = [
         pltpu.make_async_copy(
@@ -84,7 +88,18 @@
         pltpu.make_async_copy(flags, flags_here, small_sem.at[1]),
         pltpu.make_async_copy(table, table_here, small_sem.at[2]),
     ]
-    for load in small + loads[:2]:
+    for load in small:
+        load.start()
+
+    barrier = pltpu.get_barrier_semaphore()
+    for j in range(8):
+        signal(barrier, {"grid": near_peer(me, j)})
+    for d in (2, 1, 3):
+        signal(barrier, {"grid": line_peer(me, d)})
+        signal(barrier, {"chan": lax.rem(group + d, chan_count)})
+    signal(barrier, {"grid": core_mate(me)})
+
+    for load in loads[:2]:
         load.start()
     for load in small:
         load.wait()
@@ -122,19 +137,24 @@
             device_id_type=MESH,
         ).start()
 
-    def send_ring(k):
+    def send_all(k, count, peer_at):
         def one_peer(j, carry):
-            send_to(k, z_ring_peer(me, j))
+            send_to(k, peer_at(me, j))
             return carry
 
-        lax.fori_loop(0, 15, one_peer, 0, unroll=UNROLL)
-
-    def send_others(k):
-        def one_peer(j, carry):
-            send_to(k, other_peer(me, j))
-            return carry
-
-        lax.fori_loop(0, 48, one_peer, 0, unroll=UNROLL)
+        lax.fori_loop(0, count, one_peer, 0, unroll=UNROLL)
+
+    def send_chunk(k):
+        if k < chunks - 1:
+            send_all(k, 6, far_peer)
+            send_all(k, 48, other_peer)
+            send_all(k, 8, near_peer)
+        else:
+            send_all(k, 62, last_peer)
+        send_to(k, core_mate(me))
+        keep_own(k)
+
+    def keep_own(k):
         cols[span(k), pl.ds(me, 1)] = rows[span(k), pl.ds(me, 1)]
 
     def all_copies(k):
@@ -161,12 +181,18 @@
     for load in loads[2:]:
         load.start()
     row_dft(0)
-    pl.semaphore_wait(barrier, 15 + 3 + chan_count - 1)
+    pl.semaphore_wait(barrier, 8 + 3 + chan_count - 1 + 1)
+    for dz in (2, 6, 1, 7):
+        signal(near_sem, {"grid": at_offset(me, 0, dz, me % 2)})
+    send_all(0, 8, near_peer)
+    send_to(0, core_mate(me))
+    pl.semaphore_wait(near_sem, 4)
     for d in (2, 1, 3):
         signal(ring_sem, {"grid": line_peer(me, d)})
-    send_ring(0)
+    send_all(0, 6, far_peer)
+    keep_own(0)
     pl.semaphore_wait(ring_sem, 3)
-    send_others(0)
+    send_all(0, 48, other_peer)
 
     received = 0
     for k in range(1, chunks):
@@ -175,8 +201,7 @@
             received += 1
         loads[k].wait()
         row_dft(k)
-        send_ring(k)
-        send_others(k)
+        send_chunk(k)
     for k in range(received, chunks):
         col_dft(k)
 
@@ -230,6 +255,7 @@
             pltpu.SemaphoreType.DMA((len(SIZES),)),
             pltpu.SemaphoreType.DMA((len(SIZES),)),
             pltpu.SemaphoreType.REGULAR,
+            pltpu.SemaphoreType.REGULAR,
             pltpu.SemaphoreType.DMA((chan_count - 1,)),
             pltpu.SemaphoreType.DMA((chan_count - 1,)),
         ],

time: 199 us -> 199 us (level)
  no operation moved by 1% of the time
where the time goes in v2:
time: 199 us
  Pallas kernels  199 us (100%)
    pallas_call x1, Pallas kernels, on_device(): pl.pallas_call(kernel, name='sky', out_shape=pltpu.VMEM((1, share), jnp.f...  199 us

profile of v2, /device:TPU:1, one launch (start us, length us, event | category | flops | bytes accessed | tf_op | source)
XLA Modules:
  0.0 199.0 jit_solution(5051965228357591552)
XLA Ops:
  0.0 198.5 %sky.1 = f32[1,16]{1,0:T(1,128)S(1)} custom-call(f32[2,128,64,128]{3,2,1,0:T(8,128)} %volt.1, s32[1,64]{1,0:T(1,128)} %bitcast.4, s32[1,64]{1,0:T(1,128)} %bitcast.5, f32[128,128]{1,0:T(8,128)} %constant.2.clone.table), custom_call_target="tpu_custom_call" | custom-call | tf_op jit(solution)/shard_map/sky/pallas_call | solution.py:237
  198.5 0.5 copy.6

commit v3 on v2

--- a/solution.py
+++ b/solution.py
@@ -144,14 +144,18 @@
 
         lax.fori_loop(0, count, one_peer, 0, unroll=UNROLL)
 
+    def send_near(k):
+        send_all(k, 8, near_peer)
+        send_to(k, core_mate(me))
+
     def send_chunk(k):
         if k < chunks - 1:
             send_all(k, 6, far_peer)
+            send_near(k)
             send_all(k, 48, other_peer)
-            send_all(k, 8, near_peer)
         else:
             send_all(k, 62, last_peer)
-        send_to(k, core_mate(me))
+            send_to(k, core_mate(me))
         keep_own(k)
 
     def keep_own(k):
@@ -184,18 +188,23 @@
     pl.semaphore_wait(barrier, 8 + 3 + chan_count - 1 + 1)
     for dz in (2, 6, 1, 7):
         signal(near_sem, {"grid": at_offset(me, 0, dz, me % 2)})
-    send_all(0, 8, near_peer)
-    send_to(0, core_mate(me))
+    send_near(0)
+    loads[1].wait()
+    row_dft(1)
+    send_near(1)
     pl.semaphore_wait(near_sem, 4)
     for d in (2, 1, 3):
         signal(ring_sem, {"grid": line_peer(me, d)})
-    send_all(0, 6, far_peer)
-    keep_own(0)
+    for k in (0, 1):
+        send_all(k, 6, far_peer)
+    for k in (0, 1):
+        keep_own(k)
     pl.semaphore_wait(ring_sem, 3)
-    send_all(0, 48, other_peer)
+    for k in (0, 1):
+        send_all(k, 48, other_peer)
 
     received = 0
-    for k in range(1, chunks):
+    for k in range(2, chunks):
         while STARTS[k] - STARTS[received] >= AHEAD:
             col_dft(received)
             received += 1

time: 199 us -> 199 us (level)
  no operation moved by 1% of the time
where the time goes in v3:
time: 199 us
  Pallas kernels  198 us (99%)
    pallas_call x1, Pallas kernels, on_device(): pl.pallas_call(kernel, name='sky', out_shape=pltpu.VMEM((1, share), jnp.f...  198 us

profile of v3, /device:TPU:1, one launch (start us, length us, event | category | flops | bytes accessed | tf_op | source)
XLA Modules:
  0.0 198.8 jit_solution(14174540974168087625)
XLA Ops:
  0.0 198.3 %sky.1 = f32[1,16]{1,0:T(1,128)S(1)} custom-call(f32[2,128,64,128]{3,2,1,0:T(8,128)} %volt.1, s32[1,64]{1,0:T(1,128)} %bitcast.4, s32[1,64]{1,0:T(1,128)} %bitcast.5, f32[128,128]{1,0:T(8,128)} %constant.2.clone.table), custom_call_target="tpu_custom_call" | custom-call | tf_op jit(solution)/shard_map/sky/pallas_call | solution.py:246
  198.3 0.5 copy.6

commit v4 on v3

--- a/solution.py
+++ b/solution.py
@@ -16,6 +16,7 @@
 SIZES = (8, 8, 16, 16, 16, 16, 16, 16, 8, 4, 2, 2)
 STARTS = tuple(sum(SIZES[:k]) for k in range(len(SIZES)))
 AHEAD = 64
+TAIL = 3
 UNROLL = 8
 MESH = pl.DeviceIdType.MESH
 HIGHEST = lax.Precision.HIGHEST
@@ -52,11 +53,14 @@
     return at_offset(me, 3 - j % 3, 4 + half * (1 - 2 * (rank % 2)), (j // 3) % 2)
 
 
-def last_peer(me, j):
-    core, rest = j // 31, j % 31
-    rank = rest // 4
-    half = (rank + 1) // 2
-    return at_offset(me, 3 - rest % 4, 4 + half * (1 - 2 * (rank % 2)), core)
+def tail_far_peer(me, j):
+    rank = j // 8
+    return at_offset(me, 3 - j % 4, 4 + (rank + 1) // 2 * (1 - 2 * (rank % 2)), (j // 4) % 2)
+
+
+def tail_near_peer(me, j, core):
+    rank = j // 4
+    return at_offset(me, 3 - j % 4, (2 - rank // 2) * (1 - 2 * (rank % 2)), core)
 
 
 def line_peer(me, d):
@@ -149,14 +153,20 @@
         send_to(k, core_mate(me))
 
     def send_chunk(k):
-        if k < chunks - 1:
-            send_all(k, 6, far_peer)
-            send_near(k)
-            send_all(k, 48, other_peer)
-        else:
-            send_all(k, 62, last_peer)
+        send_all(k, 6, far_peer)
+        send_near(k)
+        send_all(k, 48, other_peer)
+        keep_own(k)
+
+    def send_tail(ks):
+        for k in ks:
+            send_all(k, 24, tail_far_peer)
+        for k in ks:
             send_to(k, core_mate(me))
-        keep_own(k)
+            keep_own(k)
+        for core in (0, 1):
+            for k in ks:
+                send_all(k, 19, lambda me, j: tail_near_peer(me, j, core))
 
     def keep_own(k):
         cols[span(k), pl.ds(me, 1)] = rows[span(k), pl.ds(me, 1)]
@@ -204,13 +214,17 @@
         send_all(k, 48, other_peer)
 
     received = 0
-    for k in range(2, chunks):
+    for k in range(2, chunks - TAIL):
         while STARTS[k] - STARTS[received] >= AHEAD:
             col_dft(received)
             received += 1
         loads[k].wait()
         row_dft(k)
         send_chunk(k)
+    for k in range(chunks - TAIL, chunks):
+        loads[k].wait()
+        row_dft(k)
+    send_tail(range(chunks - TAIL, chunks))
     for k in range(received, chunks):
         col_dft(k)
 

time: 199 us -> 199 us (level)
  no operation moved by 1% of the time
where the time goes in v4:
time: 199 us
  Pallas kernels  199 us (100%)
    pallas_call x1, Pallas kernels, on_device(): pl.pallas_call(kernel, name='sky', out_shape=pltpu.VMEM((1, share), jnp.f...  199 us

profile of v4, /device:TPU:1, one launch (start us, length us, event | category | flops | bytes accessed | tf_op | source)
XLA Modules:
  0.0 199.1 jit_solution(16015110725298256622)
XLA Ops:
  0.0 198.6 %sky.1 = f32[1,16]{1,0:T(1,128)S(1)} custom-call(f32[2,128,64,128]{3,2,1,0:T(8,128)} %volt.1, s32[1,64]{1,0:T(1,128)} %bitcast.4, s32[1,64]{1,0:T(1,128)} %bitcast.5, f32[128,128]{1,0:T(8,128)} %constant.2.clone.table), custom_call_target="tpu_custom_call" | custom-call | tf_op jit(solution)/shard_map/sky/pallas_call | solution.py:260
  198.6 0.5 copy.6

commit v5 on v4

--- a/solution.py
+++ b/solution.py
@@ -61,6 +61,16 @@
 def tail_near_peer(me, j, core):
     rank = j // 4
     return at_offset(me, 3 - j % 4, (2 - rank // 2) * (1 - 2 * (rank % 2)), core)
+
+
+def starts_early(peer):
+    return (peer // 16 < 2) & (peer % 2 == 1)
+
+
+def early_peer(me, j):
+    rank = j % 8
+    z = (me // 2) % 8 + 4 + (rank + 1) // 2 * (1 - 2 * (rank % 2))
+    return j // 8 * 16 + z % 8 * 2 + 1
 
 
 def line_peer(me, d):
@@ -159,14 +169,44 @@
         keep_own(k)
 
     def send_tail(ks):
+        def send_if(k, peer, wanted):
+            @pl.when(wanted)
+            def _():
+                send_to(k, peer)
+
+        def send_far(k):
+            def one_pair(j, carry):
+                early = early_peer(me, j)
+                send_if(k, early, early // 2 != me // 2)
+                far = tail_far_peer(me, j)
+                send_if(k, far, jnp.logical_not(starts_early(far)))
+                return carry
+
+            def one_far(j, carry):
+                far = tail_far_peer(me, j)
+                send_if(k, far, jnp.logical_not(starts_early(far)))
+                return carry
+
+            lax.fori_loop(0, 16, one_pair, 0, unroll=UNROLL)
+            lax.fori_loop(16, 24, one_far, 0, unroll=UNROLL)
+
+        def send_rest(k, core):
+            def one_peer(j, carry):
+                near = tail_near_peer(me, j, core)
+                send_if(k, near, jnp.logical_not(starts_early(near)))
+                return carry
+
+            lax.fori_loop(0, 19, one_peer, 0, unroll=UNROLL)
+
         for k in ks:
-            send_all(k, 24, tail_far_peer)
+            send_far(k)
         for k in ks:
             send_to(k, core_mate(me))
             keep_own(k)
-        for core in (0, 1):
-            for k in ks:
-                send_all(k, 19, lambda me, j: tail_near_peer(me, j, core))
+        for k in ks:
+            send_all(k, 19, lambda me, j: tail_near_peer(me, j, 0))
+        for k in ks:
+            send_rest(k, 1)
 
     def keep_own(k):
         cols[span(k), pl.ds(me, 1)] = rows[span(k), pl.ds(me, 1)]

time: 199 us -> 198 us (level); the launches traced: 199 us -> 196 us
  Pallas kernels: 199 us -> 196 us
    pallas_call x1, Pallas kernels: 199 us -> 196 us  [on_device(): pl.pallas_call(kernel, name='sky', out_shape=pltpu.VMEM((1, share), jnp.f...]
where the time goes in v5:
time: 198 us; the launch traced here: 196 us
  Pallas kernels  196 us (99%)
    pallas_call x1, Pallas kernels, on_device(): pl.pallas_call(kernel, name='sky', out_shape=pltpu.VMEM((1, share), jnp.f...  196 us

profile of v5, /device:TPU:1, one launch (start us, length us, event | category | flops | bytes accessed | tf_op | source)
XLA Modules:
  0.0 196.0 jit_solution(3131798338854157556)
XLA Ops:
  0.0 195.5 %sky.1 = f32[1,16]{1,0:T(1,128)S(1)} custom-call(f32[2,128,64,128]{3,2,1,0:T(8,128)} %volt.1, s32[1,64]{1,0:T(1,128)} %bitcast.4, s32[1,64]{1,0:T(1,128)} %bitcast.5, f32[128,128]{1,0:T(8,128)} %constant.2.clone.table), custom_call_target="tpu_custom_call" | custom-call | tf_op jit(solution)/shard_map/sky/pallas_call | solution.py:300
  195.5 0.5 copy.6

commit v6 on v5

--- a/solution.py
+++ b/solution.py
@@ -63,8 +63,12 @@
     return at_offset(me, 3 - j % 4, (2 - rank // 2) * (1 - 2 * (rank % 2)), core)
 
 
+def low_x(peer):
+    return peer // 16 < 2
+
+
 def starts_early(peer):
-    return (peer // 16 < 2) & (peer % 2 == 1)
+    return low_x(peer) & (peer % 2 == 1)
 
 
 def early_peer(me, j):
@@ -190,10 +194,10 @@
             lax.fori_loop(0, 16, one_pair, 0, unroll=UNROLL)
             lax.fori_loop(16, 24, one_far, 0, unroll=UNROLL)
 
-        def send_rest(k, core):
+        def send_rest(k, core, low):
             def one_peer(j, carry):
                 near = tail_near_peer(me, j, core)
-                send_if(k, near, jnp.logical_not(starts_early(near)))
+                send_if(k, near, low_x(near) == low)
                 return carry
 
             lax.fori_loop(0, 19, one_peer, 0, unroll=UNROLL)
@@ -203,10 +207,9 @@
         for k in ks:
             send_to(k, core_mate(me))
             keep_own(k)
-        for k in ks:
-            send_all(k, 19, lambda me, j: tail_near_peer(me, j, 0))
-        for k in ks:
-            send_rest(k, 1)
+        for core, low in ((0, True), (0, False), (1, False)):
+            for k in ks:
+                send_rest(k, core, low)
 
     def keep_own(k):
         cols[span(k), pl.ds(me, 1)] = rows[span(k), pl.ds(me, 1)]

time: 198 us -> 198 us (level)
  no operation moved by 1% of the time
where the time goes in v6:
time: 198 us; the launch traced here: 196 us
  Pallas kernels  196 us (99%)
    pallas_call x1, Pallas kernels, on_device(): pl.pallas_call(kernel, name='sky', out_shape=pltpu.VMEM((1, share), jnp.f...  196 us

profile of v6, /device:TPU:1, one launch (start us, length us, event | category | flops | bytes accessed | tf_op | source)
XLA Modules:
  0.0 196.0 jit_solution(1217110613482068942)
XLA Ops:
  0.0 195.5 %sky.1 = f32[1,16]{1,0:T(1,128)S(1)} custom-call(f32[2,128,64,128]{3,2,1,0:T(8,128)} %volt.1, s32[1,64]{1,0:T(1,128)} %bitcast.4, s32[1,64]{1,0:T(1,128)} %bitcast.5, f32[128,128]{1,0:T(8,128)} %constant.2.clone.table), custom_call_target="tpu_custom_call" | custom-call | tf_op jit(solution)/shard_map/sky/pallas_call | solution.py:303
  195.5 0.5 copy.6

commit v7 on v5

--- a/solution.py
+++ b/solution.py
@@ -13,7 +13,7 @@
 CHANNELS = 512
 TIMES = 128
 LANES = 128
-SIZES = (8, 8, 16, 16, 16, 16, 16, 16, 8, 4, 2, 2)
+SIZES = (4, 8, 12, 16, 16, 16, 16, 16, 8, 8, 4, 2, 2)
 STARTS = tuple(sum(SIZES[:k]) for k in range(len(SIZES)))
 AHEAD = 64
 TAIL = 3

time: 198 us -> 197 us (level)
  no operation moved by 1% of the time
where the time goes in v7:
time: 197 us; the launch traced here: 195 us
  Pallas kernels  195 us (99%)
    pallas_call x1, Pallas kernels, on_device(): pl.pallas_call(kernel, name='sky', out_shape=pltpu.VMEM((1, share), jnp.f...  195 us

profile of v7, /device:TPU:1, one launch (start us, length us, event | category | flops | bytes accessed | tf_op | source)
XLA Modules:
  0.0 195.4 jit_solution(15819431242317370959)
XLA Ops:
  0.0 194.9 %sky.1 = f32[1,16]{1,0:T(1,128)S(1)} custom-call(f32[2,128,64,128]{3,2,1,0:T(8,128)} %volt.1, s32[1,64]{1,0:T(1,128)} %bitcast.4, s32[1,64]{1,0:T(1,128)} %bitcast.5, f32[128,128]{1,0:T(8,128)} %constant.2.clone.table), custom_call_target="tpu_custom_call" | custom-call | tf_op jit(solution)/shard_map/sky/pallas_call | solution.py:300
  194.9 0.5 copy.6

commit v8 on v7

--- a/solution.py
+++ b/solution.py
@@ -136,7 +136,7 @@
             rows[2 * t + 1] = y[GRID_COLUMNS:]
             return carry
 
-        lax.fori_loop(0, SIZES[k], one_time, 0)
+        lax.fori_loop(0, SIZES[k], one_time, 0, unroll=2)
 
     def span(k):
         return pl.ds(2 * STARTS[k], 2 * SIZES[k])
@@ -229,7 +229,7 @@
             y = jnp.dot(table_here[...], x, precision=HIGHEST, preferred_element_type=jnp.float32)
             return total + y * y
 
-        power[...] += lax.fori_loop(0, SIZES[k], one_time, jnp.zeros((2 * NROW, LANES), jnp.float32))
+        power[...] += lax.fori_loop(0, SIZES[k], one_time, jnp.zeros((2 * NROW, LANES), jnp.float32), unroll=2)
 
     loads[0].wait()
     for load in loads[2:]:

time: 197 us -> 196 us (level)
  no operation moved by 1% of the time
where the time goes in v8:
time: 196 us; the launch traced here: 195 us
  Pallas kernels  194 us (99%)
    pallas_call x1, Pallas kernels, on_device(): pl.pallas_call(kernel, name='sky', out_shape=pltpu.VMEM((1, share), jnp.f...  194 us

profile of v8, /device:TPU:1, one launch (start us, length us, event | category | flops | bytes accessed | tf_op | source)
XLA Modules:
  0.0 194.7 jit_solution(4351223622432165500)
XLA Ops:
  0.0 194.1 %sky.1 = f32[1,16]{1,0:T(1,128)S(1)} custom-call(f32[2,128,64,128]{3,2,1,0:T(8,128)} %volt.1, s32[1,64]{1,0:T(1,128)} %bitcast.4, s32[1,64]{1,0:T(1,128)} %bitcast.5, f32[128,128]{1,0:T(8,128)} %constant.2.clone.table), custom_call_target="tpu_custom_call" | custom-call | tf_op jit(solution)/shard_map/sky/pallas_call | solution.py:300
  194.1 0.5 copy.6
